TPU v7x, 32 devices: a whole 2x2x4 slice. The times are simulated.
32 devices in a mesh: groups: 2 (over y), date: 4 (over z), tile: 4 (over x, core).
Axes of the slice: x: 2, y: 2, z: 4, core: 2. Of those that a mesh axis runs over, the one named last changes fastest.
Arguments:
- acquired: float32 [2, 32, 128, 128], P(None, 'date', ('groups', 'tile')), parts along dimension 2, may hold values from -10 to 10, as said below
Outputs:
- coherence: float32 [2, 4, 32, 8, 128, 128], P(None, None, 'date', None, ('groups', 'tile')), parts along dimension 4
There are 2 independent parts, one for each index of `groups`. A program takes and returns all parts, laid end to end along the dimension named above; each array names one. Nothing has to cross between parts.
Inputs may be any that keep to these rules, and one draw needn't show every extreme that they name: `acquired`: every pixel's magnitude, the square root of the sum of its two parts squared, lies between 0.1 and 10.
All inputs are finite; a program needn't handle non-finite values.
Results may differ from a plain program's by a relative error of at most 0.000058.
Values sent between devices are 32-bit elements; how exact they have to be, the bound alone decides.
No kernel may reach another device: no remote copies, remote signals or barrier semaphores. Data moves between devices by JAX's collectives and lax.ppermute only.
A program may use at most 64 MiB of HBM per device.

v0:
```python
import jax
import jax.numpy as jnp
from jax import lax
from jax.sharding import PartitionSpec as P

SHIFTS = 4


row_reach = 5
col_reach = 2


def padded(cells, sides, width):
    for axis, dim in sides:
        count = lax.axis_size(axis)
        ends = count - 1
        head = lax.slice_in_dim(cells, 0, width, axis=dim)
        tail = lax.slice_in_dim(cells, cells.shape[dim] - width, cells.shape[dim], axis=dim)
        cells = jnp.concatenate(
            [
                lax.ppermute(tail, axis, [(i, (i + 1) % count) for i in range(ends)]),
                cells,
                lax.ppermute(head, axis, [((i + 1) % count, i) for i in range(ends)]),
            ],
            axis=dim,
        )
    return cells


def passed_along(value, axis, steps):
    count = lax.axis_size(axis)
    pairs = [(source, (source + steps) % count) for source in range(count)]
    return lax.ppermute(value, axis, pairs)


def band_tables(height, breadth):
    first = lax.broadcasted_iota(jnp.int32, (height, height + 2 * row_reach), 0)
    second = lax.broadcasted_iota(jnp.int32, (height, height + 2 * row_reach), 1)
    row_band = ((second >= first) & (second <= first + 2 * row_reach)).astype(jnp.float32)
    left = lax.broadcasted_iota(jnp.int32, (breadth, breadth), 0)
    right = lax.broadcasted_iota(jnp.int32, (breadth, breadth), 1)
    col_band = (jnp.abs(left - right) <= col_reach).astype(jnp.float32)
    return (row_band, col_band)


def box_sum(values_in, row_band, col_band):
    rows_done = jnp.einsum("ir,...rc->...ic", row_band, values_in, precision=lax.Precision.HIGHEST)
    return jnp.einsum("...ic,cd->...id", rows_done, col_band, precision=lax.Precision.HIGHEST)


def block_coherence(anchor, anchor_power, partner, partner_power, row_band, col_band):
    anchor_re = anchor[0][:, None]
    anchor_im = anchor[1][:, None]
    partner_re = partner[0][None]
    partner_im = partner[1][None]
    cross_re = box_sum(anchor_re * partner_re + anchor_im * partner_im, row_band, col_band)
    cross_im = box_sum(anchor_im * partner_re - anchor_re * partner_im, row_band, col_band)
    inverse = lax.rsqrt(anchor_power[:, None] * partner_power[None])
    return jnp.stack([cross_re * inverse, cross_im * inverse])


def on_device(acquired):
    height = acquired.shape[2]
    breadth = acquired.shape[3]
    row_band, col_band = band_tables(height, breadth)
    anchor = padded(acquired, (("tile", 2),), row_reach)
    anchor_power = box_sum(anchor[0] * anchor[0] + anchor[1] * anchor[1], row_band, col_band)
    blocks = [block_coherence(anchor, anchor_power, anchor, anchor_power, row_band, col_band)]
    travel = anchor
    for offset in range(1, SHIFTS):
        travel = passed_along(travel, "date", -1)
        partner_power = box_sum(travel[0] * travel[0] + travel[1] * travel[1], row_band, col_band)
        blocks.append(
            block_coherence(anchor, anchor_power, travel, partner_power, row_band, col_band)
        )
    return jnp.stack(blocks, axis=1)


def solution(mesh):
    in_specs = (P(None, "date", ("groups", "tile"), None),)
    out_specs = P(None, None, "date", None, ("groups", "tile"), None)
    return jax.shard_map(
        on_device, mesh=mesh, in_specs=in_specs, out_specs=out_specs, check_vma=False
    )
```

profile of v0, /device:TPU:0, one launch (start us, length us, event | category | flops | bytes accessed | tf_op | source)
XLA Modules:
  0.0 48.4 jit_solution(8435805710342757056)
XLA Ops:
  0.0 0.9 %fusion.129 = (f32[2,8,5,128]{3,2,1,0:T(8,128)S(1)}, f32[2,8,5,128]{3,2,1,0:T(8,128)S(1)}) fusion(f32[2,8,16,128]{3,2,1,0:T(8,128)} %param.1), kind=kLoop, calls=%fused_computation.159 | loop fusion | bytes 163840 | tf_op jit(solution)/shard_map/slice | solution.py:18
  0.9 2.4 %collective-permute-start = (f32[2,8,5,128]{3,2,1,0:T(8,128)S(1)}, f32[2,8,5,128]{3,2,1,0:T(8,128)S(1)}, u32[]{:S(2)}, u32[]{:S(2)}) collective-permute-start(f32[2,8,5,128]{3,2,1,0:T(8,128)S(1)} %get-tuple-element.13), channel_id=1, source_target_pairs={{0,1},{1,2},{2,3},{4,5},{5,6},{6,7},{8,9},{9,10},{10,11},{12,13},{... | collective-permute-start | bytes 122888 | tf_op jit(solution)/shard_map/ppermute | solution.py:21
  3.3 1.3 %collective-permute-start.1 = (f32[2,8,5,128]{3,2,1,0:T(8,128)S(1)}, f32[2,8,5,128]{3,2,1,0:T(8,128)S(1)}, u32[]{:S(2)}, u32[]{:S(2)}) collective-permute-start(f32[2,8,5,128]{3,2,1,0:T(8,128)S(1)} %get-tuple-element.14), channel_id=1, source_target_pairs={{1,0},{2,1},{3,2},{5,4},{6,5},{7,6},{9,8},{10,9},{11,10},{13,12},{... | collective-permute-start | bytes 122888 | tf_op jit(solution)/shard_map/ppermute | solution.py:23
  4.6 0.0 collective-permute-done
  4.6 3.9 %collective-permute-done.1 = f32[2,8,5,128]{3,2,1,0:T(8,128)S(1)} collective-permute-done((f32[2,8,5,128]{3,2,1,0:T(8,128)S(1)}, f32[2,8,5,128]{3,2,1,0:T(8,128)S(1)}, u32[]{:S(2)}, u32[]{:S(2)}) %collective-permute-start.1) | collective-permute-done | bytes 40992 | tf_op jit(solution)/shard_map/ppermute | solution.py:23
  8.5 0.9 %pad_maximum_fusion.1 = f32[2,8,26,128]{3,2,1,0:T(8,128)S(1)} fusion(f32[2,8,5,128]{3,2,1,0:T(8,128)S(1)} %collective-permute-done.1, f32[2,8,16,128]{3,2,1,0:T(8,128)} %param.1, f32[2,8,5,128]{3,2,1,0:T(8,128)S(1)} %collective-permute-done), kind=kLoop, calls=%fused_computation.93 | loop fusion | flops 106496 | bytes 425984 | tf_op jit(solution)/shard_map/concatenate | solution.py:19
  9.5 3.7 %collective-permute-start.2 = (f32[2,8,26,128]{3,2,1,0:T(8,128)S(1)}, f32[2,8,26,128]{3,2,1,0:T(8,128)S(1)}, u32[]{:S(2)}, u32[]{:S(2)}) collective-permute-start(f32[2,8,26,128]{3,2,1,0:T(8,128)S(1)} %pad_maximum_fusion.1), channel_id=1, source_target_pairs={{0,12},{4,0},{8,4},{12,8},{1,13},{5,1},{9,5},{13,9},{2,14},{6,2},{... | collective-permute-start | bytes 638984 | tf_op jit(solution)/shard_map/ppermute | solution.py:33
  13.2 0.2 convolution_bitcast_fusion.11
  13.4 0.7 %convolution_bitcast_fusion.6 = f32[8,8,16,128]{3,2,1,0:T(8,128)S(1)} fusion(f32[8,26,128]{2,1,0:T(8,128)S(1)} %get-tuple-element.10, f32[8,26,128]{2,1,0:T(8,128)S(1)} %get-tuple-element.9, s32[16]{0:T(128)S(1)} %iota_add_fusion), kind=kOutput, calls=%fused_computation.7 | convolution fusion | flops 41534688 | bytes 737344 | tf_op jit(solution)/shard_map/ir,...rc->...ic/dot_general | solution.py:47
  14.1 0.7 %convolution_bitcast_fusion.7 = f32[8,8,16,128]{3,2,1,0:T(8,128)S(1)} fusion(f32[8,26,128]{2,1,0:T(8,128)S(1)} %get-tuple-element.10, f32[8,26,128]{2,1,0:T(8,128)S(1)} %get-tuple-element.9, s32[16]{0:T(128)S(1)} %iota_add_fusion), kind=kOutput, calls=%fused_computation.8 | convolution fusion | flops 41534688 | bytes 737344 | tf_op jit(solution)/shard_map/ir,...rc->...ic/dot_general | solution.py:47
  14.7 0.2 fusion.90
  14.9 0.4 fusion.6
  15.3 0.4 fusion.7
  15.7 2.2 %collective-permute-done.2 = f32[2,8,26,128]{3,2,1,0:T(8,128)S(1)} collective-permute-done((f32[2,8,26,128]{3,2,1,0:T(8,128)S(1)}, f32[2,8,26,128]{3,2,1,0:T(8,128)S(1)}, u32[]{:S(2)}, u32[]{:S(2)}) %collective-permute-start.2) | collective-permute-done | bytes 213024 | tf_op jit(solution)/shard_map/ppermute | solution.py:33
  17.9 0.7 %convolution_bitcast_fusion.4 = f32[8,8,16,128]{3,2,1,0:T(8,128)S(1)} fusion(f32[8,26,128]{2,1,0:T(8,128)S(1)} %get-tuple-element.6, f32[8,26,128]{2,1,0:T(8,128)S(1)} %get-tuple-element.5, f32[8,26,128]{2,1,0:T(8,128)S(1)} %get-tuple-element.10, f32[8,26,128]{2,1,0:T(8,128)S(1)} %get-tuple-element.9, s32[16]{0:T(128)S(1)} %iota_add_fusion), kind=kOutput, calls=%fused_computation.5 | convolution fusion | flops 41534688 | bytes 950336 | tf_op jit(solution)/shard_map/ir,...rc->...ic/dot_general | solution.py:47
  18.6 0.7 %convolution_bitcast_fusion.5 = f32[8,8,16,128]{3,2,1,0:T(8,128)S(1)} fusion(f32[8,26,128]{2,1,0:T(8,128)S(1)} %get-tuple-element.6, f32[8,26,128]{2,1,0:T(8,128)S(1)} %get-tuple-element.5, f32[8,26,128]{2,1,0:T(8,128)S(1)} %get-tuple-element.10, f32[8,26,128]{2,1,0:T(8,128)S(1)} %get-tuple-element.9, s32[16]{0:T(128)S(1)} %iota_add_fusion), kind=kOutput, calls=%fused_computation.6 | convolution fusion | flops 41534688 | bytes 950336 | tf_op jit(solution)/shard_map/ir,...rc->...ic/dot_general | solution.py:47
  19.3 0.2 convolution_bitcast_fusion.10
  19.5 0.2 fusion.88
  19.7 0.4 fusion.4
  20.1 4.3 %collective-permute-start.3 = (f32[2,8,26,128]{3,2,1,0:T(8,128)S(1)}, f32[2,8,26,128]{3,2,1,0:T(8,128)S(1)}, u32[]{:S(2)}, u32[]{:S(2)}) collective-permute-start(f32[2,8,26,128]{3,2,1,0:T(8,128)S(1)} %collective-permute-done.2), channel_id=1, source_target_pairs={{0,12},{4,0},{8,4},{12,8},{1,13},{5,1},{9,5},{13,9},{2,14},{6,2},{... | collective-permute-start | bytes 638984 | tf_op jit(solution)/shard_map/ppermute | solution.py:33
  24.4 0.4 fusion.5
  24.8 0.1 maximum_bitcast_fusion
  25.0 5.3 %collective-permute-done.3 = f32[2,8,26,128]{3,2,1,0:T(8,128)S(1)} collective-permute-done((f32[2,8,26,128]{3,2,1,0:T(8,128)S(1)}, f32[2,8,26,128]{3,2,1,0:T(8,128)S(1)}, u32[]{:S(2)}, u32[]{:S(2)}) %collective-permute-start.3) | collective-permute-done | bytes 213024 | tf_op jit(solution)/shard_map/ppermute | solution.py:33
  30.3 0.7 %convolution_bitcast_fusion.2 = f32[8,8,16,128]{3,2,1,0:T(8,128)S(1)} fusion(f32[8,26,128]{2,1,0:T(8,128)S(1)} %get-tuple-element.8, f32[8,26,128]{2,1,0:T(8,128)S(1)} %get-tuple-element.7, f32[8,26,128]{2,1,0:T(8,128)S(1)} %get-tuple-element.10, f32[8,26,128]{2,1,0:T(8,128)S(1)} %get-tuple-element.9, s32[16]{0:T(128)S(1)} %iota_add_fusion), kind=kOutput, calls=%fused_computation.3 | convolution fusion | flops 41534688 | bytes 950336 | tf_op jit(solution)/shard_map/ir,...rc->...ic/dot_general | solution.py:47
  31.0 0.7 %convolution_bitcast_fusion.3 = f32[8,8,16,128]{3,2,1,0:T(8,128)S(1)} fusion(f32[8,26,128]{2,1,0:T(8,128)S(1)} %get-tuple-element.8, f32[8,26,128]{2,1,0:T(8,128)S(1)} %get-tuple-element.7, f32[8,26,128]{2,1,0:T(8,128)S(1)} %get-tuple-element.10, f32[8,26,128]{2,1,0:T(8,128)S(1)} %get-tuple-element.9, s32[16]{0:T(128)S(1)} %iota_add_fusion), kind=kOutput, calls=%fused_computation.4 | convolution fusion | flops 41534688 | bytes 950336 | tf_op jit(solution)/shard_map/ir,...rc->...ic/dot_general | solution.py:47
  31.7 0.2 convolution_bitcast_fusion.9
  32.0 0.2 fusion.86
  32.2 4.3 %collective-permute-start.4 = (f32[2,8,26,128]{3,2,1,0:T(8,128)S(1)}, f32[2,8,26,128]{3,2,1,0:T(8,128)S(1)}, u32[]{:S(2)}, u32[]{:S(2)}) collective-permute-start(f32[2,8,26,128]{3,2,1,0:T(8,128)S(1)} %collective-permute-done.3), channel_id=1, source_target_pairs={{0,12},{4,0},{8,4},{12,8},{1,13},{5,1},{9,5},{13,9},{2,14},{6,2},{... | collective-permute-start | bytes 638984 | tf_op jit(solution)/shard_map/ppermute | solution.py:33
  36.5 0.4 fusion.2
  36.9 0.4 fusion.3
  37.3 5.6 %collective-permute-done.4 = f32[2,8,26,128]{3,2,1,0:T(8,128)S(1)} collective-permute-done((f32[2,8,26,128]{3,2,1,0:T(8,128)S(1)}, f32[2,8,26,128]{3,2,1,0:T(8,128)S(1)}, u32[]{:S(2)}, u32[]{:S(2)}) %collective-permute-start.4) | collective-permute-done | bytes 213024 | tf_op jit(solution)/shard_map/ppermute | solution.py:33
  42.9 0.7 %convolution_bitcast_fusion = f32[8,8,16,128]{3,2,1,0:T(8,128)S(1)} fusion(f32[8,26,128]{2,1,0:T(8,128)S(1)} %get-tuple-element.12, f32[8,26,128]{2,1,0:T(8,128)S(1)} %get-tuple-element.11, f32[8,26,128]{2,1,0:T(8,128)S(1)} %get-tuple-element.10, f32[8,26,128]{2,1,0:T(8,128)S(1)} %get-tuple-element.9, s32[16]{0:T(128)S(1)} %iota_add_fusion), kind=kOutput, calls=%fused_computation.1 | convolution fusion | flops 41534688 | bytes 950336 | tf_op jit(solution)/shard_map/ir,...rc->...ic/dot_general | solution.py:47
  43.6 0.7 %convolution_bitcast_fusion.1 = f32[8,8,16,128]{3,2,1,0:T(8,128)S(1)} fusion(f32[8,26,128]{2,1,0:T(8,128)S(1)} %get-tuple-element.12, f32[8,26,128]{2,1,0:T(8,128)S(1)} %get-tuple-element.11, f32[8,26,128]{2,1,0:T(8,128)S(1)} %get-tuple-element.10, f32[8,26,128]{2,1,0:T(8,128)S(1)} %get-tuple-element.9, s32[16]{0:T(128)S(1)} %iota_add_fusion), kind=kOutput, calls=%fused_computation.2 | convolution fusion | flops 41534688 | bytes 950336 | tf_op jit(solution)/shard_map/ir,...rc->...ic/dot_general | solution.py:47
  44.3 0.2 convolution_bitcast_fusion.8
  44.5 0.2 fusion.84
  44.7 0.4 fusion
  45.1 0.4 fusion.1
  45.5 0.1 maximum_bitcast_fusion.2
  45.6 0.5 %pad_maximum_fusion = f32[2,4,8,8,16,128]{5,4,3,2,0,1:T(8,128)S(1)} fusion(f32[2,1,8,8,16,128]{5,4,3,2,0,1:T(8,128)S(1)} %get-tuple-element.18, f32[2,1,8,8,16,128]{5,4,3,2,0,1:T(8,128)S(1)} %get-tuple-element.17, f32[2,1,8,8,16,128]{5,4,3,2,0,1:T(8,128)S(1)} %get-tuple-element.16, f32[2,1,8,8,16,128]{5,4,3,2,0,1:T(8,128)S(1)} %get-tuple-element.15), kind=kLoop, calls=%fused_computation | loop fusion | flops 3145728 | bytes 8388608 | tf_op jit(solution)/shard_map/stack | solution.py:76
  46.1 2.3 %copy.2 = f32[2,4,8,8,16,128]{5,4,3,2,1,0:T(8,128)} copy(f32[2,4,8,8,16,128]{5,4,3,2,0,1:T(8,128)S(1)} %pad_maximum_fusion) | data formatting | bytes 8388608 | tf_op jit(solution)/shard_map/stack | solution.py:76
  (5 shorter events, 0.1 us)
Async XLA Ops:
  0.9 3.7 %collective-permute-start = (f32[2,8,5,128]{3,2,1,0:T(8,128)S(1)}, f32[2,8,5,128]{3,2,1,0:T(8,128)S(1)}, u32[]{:S(2)}, u32[]{:S(2)}) collective-permute-start(f32[2,8,5,128]{3,2,1,0:T(8,128)S(1)} %get-tuple-element.13), channel_id=1, source_target_pairs={{0,1},{1,2},{2,3},{4,5},{5,6},{6,7},{8,9},{9,10},{10,11},{12,13},{... | collective-permute-start | bytes 122888 | tf_op jit(solution)/shard_map/ppermute | solution.py:21
  3.3 5.2 %collective-permute-start.1 = (f32[2,8,5,128]{3,2,1,0:T(8,128)S(1)}, f32[2,8,5,128]{3,2,1,0:T(8,128)S(1)}, u32[]{:S(2)}, u32[]{:S(2)}) collective-permute-start(f32[2,8,5,128]{3,2,1,0:T(8,128)S(1)} %get-tuple-element.14), channel_id=1, source_target_pairs={{1,0},{2,1},{3,2},{5,4},{6,5},{7,6},{9,8},{10,9},{11,10},{13,12},{... | collective-permute-start | bytes 122888 | tf_op jit(solution)/shard_map/ppermute | solution.py:23
  9.5 8.4 %collective-permute-start.2 = (f32[2,8,26,128]{3,2,1,0:T(8,128)S(1)}, f32[2,8,26,128]{3,2,1,0:T(8,128)S(1)}, u32[]{:S(2)}, u32[]{:S(2)}) collective-permute-start(f32[2,8,26,128]{3,2,1,0:T(8,128)S(1)} %pad_maximum_fusion.1), channel_id=1, source_target_pairs={{0,12},{4,0},{8,4},{12,8},{1,13},{5,1},{9,5},{13,9},{2,14},{6,2},{... | collective-permute-start | bytes 638984 | tf_op jit(solution)/shard_map/ppermute | solution.py:33
  20.1 10.2 %collective-permute-start.3 = (f32[2,8,26,128]{3,2,1,0:T(8,128)S(1)}, f32[2,8,26,128]{3,2,1,0:T(8,128)S(1)}, u32[]{:S(2)}, u32[]{:S(2)}) collective-permute-start(f32[2,8,26,128]{3,2,1,0:T(8,128)S(1)} %collective-permute-done.2), channel_id=1, source_target_pairs={{0,12},{4,0},{8,4},{12,8},{1,13},{5,1},{9,5},{13,9},{2,14},{6,2},{... | collective-permute-start | bytes 638984 | tf_op jit(solution)/shard_map/ppermute | solution.py:33
  32.2 10.7 %collective-permute-start.4 = (f32[2,8,26,128]{3,2,1,0:T(8,128)S(1)}, f32[2,8,26,128]{3,2,1,0:T(8,128)S(1)}, u32[]{:S(2)}, u32[]{:S(2)}) collective-permute-start(f32[2,8,26,128]{3,2,1,0:T(8,128)S(1)} %collective-permute-done.3), channel_id=1, source_target_pairs={{0,12},{4,0},{8,4},{12,8},{1,13},{5,1},{9,5},{13,9},{2,14},{6,2},{... | collective-permute-start | bytes 638984 | tf_op jit(solution)/shard_map/ppermute | solution.py:33
where the time goes:
time: 48.6 us; the launch traced here: 48.4 us
  waiting for transfers between devices  17 us (35%)
  starting transfers between devices  16 us (33%)
  matrix products  10.2 us (21%)
  local copies, waits for them, and re-layouts  3.27 us (7%)
  other arithmetic  1.7 us (3%)
    ppermute x3, waiting for transfers between devices, passed_along(): return lax.ppermute(value, axis, pairs)  13.1 us
    ppermute x3, starting transfers between devices, passed_along(): return lax.ppermute(value, axis, pairs)  12.3 us
    dot_general x12, matrix products, box_sum(): jnp.einsum('ir,...rc->...ic', row_band, values_in, precision=lax.Precisio...  6.33 us
    ppermute x1, waiting for transfers between devices, padded(): lax.ppermute(head, axis, [((i + 1) % count, i) for i in range(ends)])  3.92 us
    dot_general x12, matrix products, box_sum(): jnp.einsum('...ic,cd->...id', rows_done, col_band, precision=lax.Precisio...  3.85 us
    ppermute x1, starting transfers between devices, padded(): lax.ppermute(tail, axis, [(i, (i + 1) % count) for i in range(ends)])  2.4 us
    another operation x1, local copies, waits for them, and re-layouts, on_device(): return jnp.stack(blocks, axis=1)  2.32 us
    ppermute x1, starting transfers between devices, padded(): lax.ppermute(head, axis, [((i + 1) % count, i) for i in range(ends)])  1.29 us
  transfers between devices with their start and end apart: 5, of which 4 were waited for; matrix products, arithmetic and copies ran while one was open for 8% of the time, Pallas kernels for 0%

commit v1 on v0

v1 whole, which is shorter than its diff:
```python
import jax
import jax.numpy as jnp
from jax import lax
from jax.experimental import pallas as pl
from jax.experimental.pallas import tpu as pltpu
from jax.sharding import PartitionSpec as P

SHIFTS = 4

row_reach = 5
col_reach = 2


def window_sums(rows, reach, count):
    total = len(rows)
    suffix, prefix = {}, {}
    for start in range(0, total, reach):
        stop = min(start + reach, total)
        prefix[start] = rows[start]
        for i in range(start + 1, stop):
            prefix[i] = prefix[i - 1] + rows[i]
        if stop - start == reach:
            suffix[stop - 1] = rows[stop - 1]
            for i in range(stop - 2, start, -1):
                suffix[i] = suffix[i + 1] + rows[i]
    out = []
    for i in range(count):
        if i % reach == 0:
            out.append(prefix[i + reach - 1])
        else:
            out.append(suffix[i] + prefix[i + reach - 1])
    return out


def column_sums(rows, band):
    value = jnp.concatenate(rows, axis=0)
    high = value.astype(jnp.bfloat16)
    low = (value - high.astype(jnp.float32)).astype(jnp.bfloat16)
    return jnp.dot(
        jnp.concatenate([high, low], axis=1), band, preferred_element_type=jnp.float32
    )


def kernel_body(
    blocks, axis, edge_ref, mid_ref, even_ref, odd_ref, out_ref, halo, inverse, band_ref
):
    dates = edge_ref.shape[3]
    breadth = edge_ref.shape[4]
    inner = mid_ref.shape[1]
    height = inner + 2 * row_reach
    reach = 2 * row_reach + 1
    here = lax.axis_index(axis)
    count = lax.axis_size(axis)
    odd_tile = lax.rem(here, 2)

    left = lax.rem(lax.broadcasted_iota(jnp.int32, (2 * breadth, breadth), 0), breadth)
    right = lax.broadcasted_iota(jnp.int32, (2 * breadth, breadth), 1)
    band_ref[...] = (jnp.abs(left - right) <= col_reach).astype(jnp.bfloat16)
    band = band_ref[...]

    even_live = jnp.where(here == count - 1, odd_tile, 1) == 1
    odd_live = jnp.where(odd_tile == 0, here > 0, here < count - 1)
    for k in range(blocks):
        even = even_ref[k]
        odd = odd_ref[k]
        halo[k, 1 - odd_tile] = jnp.where(even_live, even, jnp.zeros_like(even))
        halo[k, odd_tile] = jnp.where(odd_live, odd, jnp.zeros_like(odd))

    def row(k, r, part, date=None):
        at = slice(None) if date is None else pl.ds(date, 1)
        if r < row_reach:
            return halo[k, 0, r, part, at, :]
        if r < 2 * row_reach:
            return edge_ref[k, r - row_reach, part, at, :]
        if r < 2 * row_reach + inner:
            return mid_ref[k, r - 2 * row_reach, part, at, :]
        if r < 3 * row_reach + inner:
            return edge_ref[k, r - row_reach - inner, part, at, :]
        return halo[k, 1, r - 3 * row_reach - inner, part, at, :]

    extent = height + 2 * row_reach
    for k in range(blocks):
        squares = []
        for r in range(extent):
            re, im = row(k, r, 0), row(k, r, 1)
            squares.append(re * re + im * im)
        power = column_sums(window_sums(squares, reach, height), band)
        inverse[k] = lax.rsqrt(power).reshape(height, dates, breadth)

    for k in range(blocks):

        def one_date(d, carry, k=k):
            real, imag = [], []
            for r in range(extent):
                a_re = jnp.broadcast_to(row(0, r, 0, d), (dates, breadth))
                a_im = jnp.broadcast_to(row(0, r, 1, d), (dates, breadth))
                b_re, b_im = row(k, r, 0), row(k, r, 1)
                real.append(a_re * b_re + a_im * b_im)
                imag.append(a_im * b_re - a_re * b_im)
            for part, values in ((0, real), (1, imag)):
                sums = column_sums(window_sums(values, reach, height), band)
                for r in range(height):
                    scale = inverse[0, r, pl.ds(d, 1), :] * inverse[k, r]
                    out_ref[part, k, d, pl.ds(r, dates, stride=height), :] = (
                        sums[r * dates : (r + 1) * dates] * scale
                    )
            return carry

        lax.fori_loop(0, dates, one_date, 0)


def coherence_of(axis, edge, mid, even, odd):
    blocks, _, _, dates, breadth = edge.shape
    height = mid.shape[1] + 2 * row_reach

    def body(*refs):
        kernel_body(blocks, axis, *refs)

    pairs = blocks * dates * dates * height * breadth
    return pl.pallas_call(
        body,
        out_shape=jax.ShapeDtypeStruct(
            (2, blocks, dates, dates * height, breadth), jnp.float32
        ),
        in_specs=[pl.BlockSpec(memory_space=pltpu.VMEM)] * 4,
        out_specs=pl.BlockSpec(memory_space=pltpu.VMEM),
        scratch_shapes=[
            pltpu.VMEM((blocks, 2, row_reach, 2, dates, breadth), jnp.float32),
            pltpu.VMEM((blocks, height, dates, breadth), jnp.float32),
            pltpu.VMEM((2 * breadth, breadth), jnp.bfloat16),
        ],
        cost_estimate=pl.CostEstimate(
            flops=pairs * 40, bytes_accessed=pairs * 8, transcendentals=0
        ),
    )(edge, mid, even, odd)


def passed_along(value, axis, steps):
    count = lax.axis_size(axis)
    pairs = [(source, (source + steps) % count) for source in range(count)]
    return lax.ppermute(value, axis, pairs)


def swapped(value, axis, first):
    count = lax.axis_size(axis)
    pairs = []
    for i in range(first, count - 1, 2):
        pairs += [(i, i + 1), (i + 1, i)]
    if first and count % 2 == 0 and count > 2:
        pairs += [(0, count - 1), (count - 1, 0)]
    return lax.ppermute(value, axis, pairs)


def on_device(acquired):
    height = acquired.shape[2]
    by_row = jnp.transpose(acquired, (2, 0, 1, 3))
    edge = jnp.concatenate([by_row[:row_reach], by_row[height - row_reach :]], axis=0)
    mid = by_row[row_reach : height - row_reach]
    edges = jnp.stack([edge] + [passed_along(edge, "date", -s) for s in range(1, SHIFTS)])
    mids = jnp.stack([mid] + [passed_along(mid, "date", -s) for s in range(1, SHIFTS)])
    odd_tile = lax.rem(lax.axis_index("tile"), 2)
    tops, bottoms = edges[:, :row_reach], edges[:, row_reach:]
    even = swapped(jnp.where(odd_tile == 0, bottoms, tops), "tile", 0)
    odd = swapped(jnp.where(odd_tile == 1, bottoms, tops), "tile", 1)
    found = coherence_of("tile", edges, mids, even, odd)
    parts, shifts, dates = found.shape[:3]
    return found.reshape(parts, shifts, dates, dates, height, found.shape[-1])


def solution(mesh):
    in_specs = (P(None, "date", ("groups", "tile"), None),)
    out_specs = P(None, None, "date", None, ("groups", "tile"), None)
    return jax.shard_map(
        on_device, mesh=mesh, in_specs=in_specs, out_specs=out_specs, check_vma=False
    )
```

time: 48.6 us -> 32 us (0.66)
  the two profiles are of different devices: /device:TPU:0 before, /device:TPU:17 now
where the time goes in v1:
time: 32 us; the launch traced here: 31.8 us
  starting transfers between devices  12.4 us (39%)
  Pallas kernels  9.88 us (31%)
  waiting for transfers between devices  6.42 us (20%)
  local copies, waits for them, and re-layouts  2.3 us (7%)
  other arithmetic  0.76 us (2%)
    ppermute x6, starting transfers between devices, passed_along(): return lax.ppermute(value, axis, pairs)  10.4 us
    pallas_call x1, Pallas kernels, coherence_of(): pl.pallas_call(body, out_shape=jax.ShapeDtypeStruct((2, blocks, dates, da...  9.88 us
    ppermute x2, waiting for transfers between devices, swapped(): return lax.ppermute(value, axis, pairs)  4.19 us
    unnamed x7, local copies, waits for them, and re-layouts  2.29 us
    ppermute x6, waiting for transfers between devices, passed_along(): return lax.ppermute(value, axis, pairs)  2.22 us
    ppermute x2, starting transfers between devices, swapped(): return lax.ppermute(value, axis, pairs)  1.96 us
    another operation x1, other arithmetic, on_device(): jnp.stack([mid] + [passed_along(mid, 'date', -s) for s in range(1, SHIFTS)])  0.69 us
  transfers between devices with their start and end apart: 8, of which 3 were waited for; matrix products, arithmetic and copies ran while one was open for 2% of the time, Pallas kernels for 0%

profile of v1, /device:TPU:17, one launch (start us, length us, event | category | flops | bytes accessed | tf_op | source)
XLA Modules:
  0.0 31.8 jit_solution(15078395996720028110)
XLA Ops:
  0.0 0.9 %copy.4 = f32[2,8,16,128]{3,1,0,2:T(8,128)S(1)} copy(f32[2,8,16,128]{3,2,1,0:T(8,128)} %param.1) | data formatting | bytes 262144 | tf_op args[0]
  1.0 0.1 collective-permute-start.1
  1.1 2.5 %collective-permute-start = (f32[10,2,8,128]{3,2,1,0:T(8,128)S(1)}, f32[10,2,8,128]{3,2,1,0:T(8,128)S(1)}, u32[]{:S(2)}, u32[]{:S(2)}) collective-permute-start(f32[10,2,8,128]{3,2,1,0:T(8,128)S(1)} %get-tuple-element.12), channel_id=1, source_target_pairs={{0,12},{4,0},{8,4},{12,8},{1,13},{5,1},{9,5},{13,9},{2,14},{6,2},{... | collective-permute-start | bytes 245768 | tf_op jit(solution)/shard_map/ppermute | solution.py:141
  3.5 0.0 collective-permute-start.2
  3.5 1.4 %collective-permute-start.4 = (f32[6,2,8,128]{3,2,1,0:T(8,128)S(1)}, f32[6,2,8,128]{3,2,1,0:T(8,128)S(1)}, u32[]{:S(2)}, u32[]{:S(2)}) collective-permute-start(f32[6,2,8,128]{3,2,1,0:T(8,128)S(1)} %get-tuple-element.8), channel_id=1, source_target_pairs={{0,8},{4,12},{8,0},{12,4},{1,9},{5,13},{9,1},{13,5},{2,10},{6,14},... | collective-permute-start | bytes 147464 | tf_op jit(solution)/shard_map/ppermute | solution.py:141
  5.0 2.0 %collective-permute-start.3 = (f32[6,2,8,128]{3,2,1,0:T(8,128)S(1)}, f32[6,2,8,128]{3,2,1,0:T(8,128)S(1)}, u32[]{:S(2)}, u32[]{:S(2)}) collective-permute-start(f32[6,2,8,128]{3,2,1,0:T(8,128)S(1)} %get-tuple-element.8), channel_id=1, source_target_pairs={{0,12},{4,0},{8,4},{12,8},{1,13},{5,1},{9,5},{13,9},{2,14},{6,2},{... | collective-permute-start | bytes 147464 | tf_op jit(solution)/shard_map/ppermute | solution.py:141
  6.9 0.0 collective-permute-done.1
  6.9 4.5 %collective-permute-start.5 = (f32[6,2,8,128]{3,2,1,0:T(8,128)S(1)}, f32[6,2,8,128]{3,2,1,0:T(8,128)S(1)}, u32[]{:S(2)}, u32[]{:S(2)}) collective-permute-start(f32[6,2,8,128]{3,2,1,0:T(8,128)S(1)} %get-tuple-element.8), channel_id=1, source_target_pairs={{0,4},{4,8},{8,12},{12,0},{1,5},{5,9},{9,13},{13,1},{2,6},{6,10},{... | collective-permute-start | bytes 147464 | tf_op jit(solution)/shard_map/ppermute | solution.py:141
  11.4 0.0 collective-permute-done
  11.4 2.1 %collective-permute-done.2 = f32[10,2,8,128]{3,2,1,0:T(8,128)S(1)} collective-permute-done((f32[10,2,8,128]{3,2,1,0:T(8,128)S(1)}, f32[10,2,8,128]{3,2,1,0:T(8,128)S(1)}, u32[]{:S(2)}, u32[]{:S(2)}) %collective-permute-start.2) | collective-permute-done | bytes 81952 | tf_op jit(solution)/shard_map/ppermute | solution.py:141
  13.6 0.0 copy-start
  13.7 2.0 %collective-permute-start.7 = (f32[4,5,2,8,128]{4,3,2,1,0:T(8,128)S(1)}, f32[4,5,2,8,128]{4,3,2,1,0:T(8,128)S(1)}, u32[]{:S(2)}, u32[]{:S(2)}) collective-permute-start(f32[4,5,2,8,128]{4,3,2,1,0:T(8,128)S(1)} %get-tuple-element.5), channel_id=1, source_target_pairs={{1,2},{2,1},{0,3},{3,0},{5,6},{6,5},{4,7},{7,4},{9,10},{10,9},{8,1... | collective-permute-start | bytes 491528 | tf_op jit(solution)/shard_map/ppermute | solution.py:151
  15.6 0.0 collective-permute-start.6
  15.6 0.0 collective-permute-done.4
  15.6 0.0 collective-permute-done.3
  15.6 0.1 collective-permute-done.5
  15.7 0.7 %pad_maximum_fusion.1.refs_1_ = f32[4,6,2,8,128]{4,3,2,1,0:T(8,128)} fusion(f32[1,6,2,8,128]{4,3,2,1,0:T(8,128)S(1)} %bitcast.21, f32[1,6,2,8,128]{4,3,2,1,0:T(8,128)S(1)} %bitcast.19, f32[1,6,2,8,128]{4,3,2,1,0:T(8,128)S(1)} %bitcast.20, f32[1,6,2,8,128]{4,3,2,1,0:T(8,128)S(1)} %get-tuple-element.7), kind=kLoop, calls=%fused_computation.1 | loop fusion | flops 147456 | bytes 393216 | tf_op jit(solution)/shard_map/stack | solution.py:160
  16.4 4.2 %collective-permute-done.7.refs_3_ = f32[4,5,2,8,128]{4,3,2,1,0:T(8,128)S(1)} collective-permute-done((f32[4,5,2,8,128]{4,3,2,1,0:T(8,128)S(1)}, f32[4,5,2,8,128]{4,3,2,1,0:T(8,128)S(1)}, u32[]{:S(2)}, u32[]{:S(2)}) %collective-permute-start.7) | collective-permute-done | bytes 163872 | tf_op jit(solution)/shard_map/ppermute | solution.py:151
  20.6 0.0 copy-start.1
  20.6 0.0 collective-permute-done.6.refs_2_
  20.6 0.0 copy-done
  20.6 0.7 %copy-done.1 = f32[4,5,2,8,128]{4,3,2,1,0:T(8,128)} copy-done((f32[4,5,2,8,128]{4,3,2,1,0:T(8,128)}, f32[4,5,2,8,128]{4,3,2,1,0:T(8,128)S(1)}, u32[]{:S(2)}) %copy-start.1) | copy-done | bytes 163864
  21.3 0.0 copy-start.2
  21.3 0.7 %copy-done.2 = f32[4,5,2,8,128]{4,3,2,1,0:T(8,128)} copy-done((f32[4,5,2,8,128]{4,3,2,1,0:T(8,128)}, f32[4,5,2,8,128]{4,3,2,1,0:T(8,128)S(1)}, u32[]{:S(2)}) %copy-start.2) | copy-done | bytes 163864
  21.9 9.9 %shard_map.17 = f32[2,4,8,128,128]{4,3,2,1,0:T(8,128)} custom-call(f32[4,10,2,8,128]{4,3,2,1,0:T(8,128)} %copy-done, f32[4,6,2,8,128]{4,3,2,1,0:T(8,128)} %pad_maximum_fusion.1.refs_1_, f32[4,5,2,8,128]{4,3,2,1,0:T(8,128)} %copy-done.2, f32[4,5,2,8,128]{4,3,2,1,0:T(8,128)} %copy-done.1), custom_call_target="tpu_custom_call" | custom-call | flops 20971520 | bytes 4194304 | tf_op jit(solution)/shard_map/pallas_call | solution.py:120
  (5 shorter events, 0.1 us)
Async XLA Ops:
  1.0 5.9 %collective-permute-start.1 = (f32[10,2,8,128]{3,2,1,0:T(8,128)S(1)}, f32[10,2,8,128]{3,2,1,0:T(8,128)S(1)}, u32[]{:S(2)}, u32[]{:S(2)}) collective-permute-start(f32[10,2,8,128]{3,2,1,0:T(8,128)S(1)} %get-tuple-element.12), channel_id=1, source_target_pairs={{0,8},{4,12},{8,0},{12,4},{1,9},{5,13},{9,1},{13,5},{2,10},{6,14},... | collective-permute-start | bytes 245768 | tf_op jit(solution)/shard_map/ppermute | solution.py:141
  1.1 10.4 %collective-permute-start = (f32[10,2,8,128]{3,2,1,0:T(8,128)S(1)}, f32[10,2,8,128]{3,2,1,0:T(8,128)S(1)}, u32[]{:S(2)}, u32[]{:S(2)}) collective-permute-start(f32[10,2,8,128]{3,2,1,0:T(8,128)S(1)} %get-tuple-element.12), channel_id=1, source_target_pairs={{0,12},{4,0},{8,4},{12,8},{1,13},{5,1},{9,5},{13,9},{2,14},{6,2},{... | collective-permute-start | bytes 245768 | tf_op jit(solution)/shard_map/ppermute | solution.py:141
  3.5 10.1 %collective-permute-start.2 = (f32[10,2,8,128]{3,2,1,0:T(8,128)S(1)}, f32[10,2,8,128]{3,2,1,0:T(8,128)S(1)}, u32[]{:S(2)}, u32[]{:S(2)}) collective-permute-start(f32[10,2,8,128]{3,2,1,0:T(8,128)S(1)} %get-tuple-element.12), channel_id=1, source_target_pairs={{0,4},{4,8},{8,12},{12,0},{1,5},{5,9},{9,13},{13,1},{2,6},{6,10},{... | collective-permute-start | bytes 245768 | tf_op jit(solution)/shard_map/ppermute | solution.py:141
  3.5 12.1 %collective-permute-start.4 = (f32[6,2,8,128]{3,2,1,0:T(8,128)S(1)}, f32[6,2,8,128]{3,2,1,0:T(8,128)S(1)}, u32[]{:S(2)}, u32[]{:S(2)}) collective-permute-start(f32[6,2,8,128]{3,2,1,0:T(8,128)S(1)} %get-tuple-element.8), channel_id=1, source_target_pairs={{0,8},{4,12},{8,0},{12,4},{1,9},{5,13},{9,1},{13,5},{2,10},{6,14},... | collective-permute-start | bytes 147464 | tf_op jit(solution)/shard_map/ppermute | solution.py:141
  5.0 10.7 %collective-permute-start.3 = (f32[6,2,8,128]{3,2,1,0:T(8,128)S(1)}, f32[6,2,8,128]{3,2,1,0:T(8,128)S(1)}, u32[]{:S(2)}, u32[]{:S(2)}) collective-permute-start(f32[6,2,8,128]{3,2,1,0:T(8,128)S(1)} %get-tuple-element.8), channel_id=1, source_target_pairs={{0,12},{4,0},{8,4},{12,8},{1,13},{5,1},{9,5},{13,9},{2,14},{6,2},{... | collective-permute-start | bytes 147464 | tf_op jit(solution)/shard_map/ppermute | solution.py:141
  6.9 8.8 %collective-permute-start.5 = (f32[6,2,8,128]{3,2,1,0:T(8,128)S(1)}, f32[6,2,8,128]{3,2,1,0:T(8,128)S(1)}, u32[]{:S(2)}, u32[]{:S(2)}) collective-permute-start(f32[6,2,8,128]{3,2,1,0:T(8,128)S(1)} %get-tuple-element.8), channel_id=1, source_target_pairs={{0,4},{4,8},{8,12},{12,0},{1,5},{5,9},{9,13},{13,1},{2,6},{6,10},{... | collective-permute-start | bytes 147464 | tf_op jit(solution)/shard_map/ppermute | solution.py:141
  13.6 7.0 %copy-start = (f32[4,10,2,8,128]{4,3,2,1,0:T(8,128)}, f32[4,10,2,8,128]{4,3,2,1,0:T(8,128)S(1)}, u32[]{:S(2)}) copy-start(f32[4,10,2,8,128]{4,3,2,1,0:T(8,128)S(1)} %pad_maximum_fusion.refs_0_) | copy-start | bytes 983044
  13.7 6.9 %collective-permute-start.7 = (f32[4,5,2,8,128]{4,3,2,1,0:T(8,128)S(1)}, f32[4,5,2,8,128]{4,3,2,1,0:T(8,128)S(1)}, u32[]{:S(2)}, u32[]{:S(2)}) collective-permute-start(f32[4,5,2,8,128]{4,3,2,1,0:T(8,128)S(1)} %get-tuple-element.5), channel_id=1, source_target_pairs={{1,2},{2,1},{0,3},{3,0},{5,6},{6,5},{4,7},{7,4},{9,10},{10,9},{8,1... | collective-permute-start | bytes 491528 | tf_op jit(solution)/shard_map/ppermute | solution.py:151
  15.6 5.0 %collective-permute-start.6 = (f32[4,5,2,8,128]{4,3,2,1,0:T(8,128)S(1)}, f32[4,5,2,8,128]{4,3,2,1,0:T(8,128)S(1)}, u32[]{:S(2)}, u32[]{:S(2)}) collective-permute-start(f32[4,5,2,8,128]{4,3,2,1,0:T(8,128)S(1)} %get-tuple-element.6), channel_id=1, source_target_pairs={{0,1},{1,0},{2,3},{3,2},{4,5},{5,4},{6,7},{7,6},{8,9},{9,8},{10,11... | collective-permute-start | bytes 491528 | tf_op jit(solution)/shard_map/ppermute | solution.py:151
  20.6 0.7 %copy-start.1 = (f32[4,5,2,8,128]{4,3,2,1,0:T(8,128)}, f32[4,5,2,8,128]{4,3,2,1,0:T(8,128)S(1)}, u32[]{:S(2)}) copy-start(f32[4,5,2,8,128]{4,3,2,1,0:T(8,128)S(1)} %collective-permute-done.7.refs_3_) | copy-start | bytes 491524
  21.3 0.7 %copy-start.2 = (f32[4,5,2,8,128]{4,3,2,1,0:T(8,128)}, f32[4,5,2,8,128]{4,3,2,1,0:T(8,128)S(1)}, u32[]{:S(2)}) copy-start(f32[4,5,2,8,128]{4,3,2,1,0:T(8,128)S(1)} %collective-permute-done.6.refs_2_) | copy-start | bytes 491524

commit v2 on v1

--- a/solution.py
+++ b/solution.py
@@ -41,12 +41,11 @@
     )
 
 
-def kernel_body(
-    blocks, axis, edge_ref, mid_ref, even_ref, odd_ref, out_ref, halo, inverse, band_ref
-):
-    dates = edge_ref.shape[3]
-    breadth = edge_ref.shape[4]
-    inner = mid_ref.shape[1]
+def kernel_body(blocks, axis, groups, unroll, *refs):
+    edge_refs, mid_refs = refs[:blocks], refs[blocks : 2 * blocks]
+    even_ref, odd_ref, out_ref, halo, inverse, found, sems = refs[2 * blocks :]
+    _, _, dates, breadth = edge_refs[0].shape
+    inner = mid_refs[0].shape[0]
     height = inner + 2 * row_reach
     reach = 2 * row_reach + 1
     here = lax.axis_index(axis)
@@ -55,8 +54,7 @@
 
     left = lax.rem(lax.broadcasted_iota(jnp.int32, (2 * breadth, breadth), 0), breadth)
     right = lax.broadcasted_iota(jnp.int32, (2 * breadth, breadth), 1)
-    band_ref[...] = (jnp.abs(left - right) <= col_reach).astype(jnp.bfloat16)
-    band = band_ref[...]
+    band = (jnp.abs(left - right) <= col_reach).astype(jnp.bfloat16)
 
     even_live = jnp.where(here == count - 1, odd_tile, 1) == 1
     odd_live = jnp.where(odd_tile == 0, here > 0, here < count - 1)
@@ -71,11 +69,11 @@
         if r < row_reach:
             return halo[k, 0, r, part, at, :]
         if r < 2 * row_reach:
-            return edge_ref[k, r - row_reach, part, at, :]
+            return edge_refs[k][r - row_reach, part, at, :]
         if r < 2 * row_reach + inner:
-            return mid_ref[k, r - 2 * row_reach, part, at, :]
+            return mid_refs[k][r - 2 * row_reach, part, at, :]
         if r < 3 * row_reach + inner:
-            return edge_ref[k, r - row_reach - inner, part, at, :]
+            return edge_refs[k][r - row_reach - inner, part, at, :]
         return halo[k, 1, r - 3 * row_reach - inner, part, at, :]
 
     extent = height + 2 * row_reach
@@ -87,6 +85,8 @@
         power = column_sums(window_sums(squares, reach, height), band)
         inverse[k] = lax.rsqrt(power).reshape(height, dates, breadth)
 
+    copies = []
+    step = dates // groups
     for k in range(blocks):
 
         def one_date(d, carry, k=k):
@@ -101,38 +101,50 @@
                 sums = column_sums(window_sums(values, reach, height), band)
                 for r in range(height):
                     scale = inverse[0, r, pl.ds(d, 1), :] * inverse[k, r]
-                    out_ref[part, k, d, pl.ds(r, dates, stride=height), :] = (
+                    found[part, k, d, pl.ds(r, dates, stride=height), :] = (
                         sums[r * dates : (r + 1) * dates] * scale
                     )
             return carry
 
-        lax.fori_loop(0, dates, one_date, 0)
+        for g in range(groups):
+            lax.fori_loop(g * step, (g + 1) * step, one_date, 0, unroll=min(unroll, step))
+            for part in range(2):
+                span = pl.ds(g * step, step)
+                copy = pltpu.make_async_copy(
+                    found.at[part, k, span], out_ref.at[part, k, span], sems.at[k, g, part]
+                )
+                copy.start()
+                copies.append(copy)
+    for copy in copies:
+        copy.wait()
 
 
-def coherence_of(axis, edge, mid, even, odd):
-    blocks, _, _, dates, breadth = edge.shape
-    height = mid.shape[1] + 2 * row_reach
+def coherence_of(axis, edges, mids, even, odd, groups=2, unroll=4):
+    blocks = len(edges)
+    _, _, dates, breadth = edges[0].shape
+    height = mids[0].shape[0] + 2 * row_reach
 
     def body(*refs):
-        kernel_body(blocks, axis, *refs)
+        kernel_body(blocks, axis, groups, unroll, *refs)
 
     pairs = blocks * dates * dates * height * breadth
+    result = (2, blocks, dates, dates * height, breadth)
     return pl.pallas_call(
         body,
-        out_shape=jax.ShapeDtypeStruct(
-            (2, blocks, dates, dates * height, breadth), jnp.float32
-        ),
-        in_specs=[pl.BlockSpec(memory_space=pltpu.VMEM)] * 4,
-        out_specs=pl.BlockSpec(memory_space=pltpu.VMEM),
+        out_shape=jax.ShapeDtypeStruct(result, jnp.float32),
+        in_specs=[pl.BlockSpec(memory_space=pltpu.VMEM)] * (2 * blocks + 2),
+        out_specs=pl.BlockSpec(memory_space=pl.ANY),
         scratch_shapes=[
             pltpu.VMEM((blocks, 2, row_reach, 2, dates, breadth), jnp.float32),
             pltpu.VMEM((blocks, height, dates, breadth), jnp.float32),
-            pltpu.VMEM((2 * breadth, breadth), jnp.bfloat16),
+            pltpu.VMEM(result, jnp.float32),
+            pltpu.SemaphoreType.DMA((blocks, groups, 2)),
         ],
+        compiler_params=pltpu.CompilerParams(vmem_limit_bytes=16 * 1024 * 1024),
         cost_estimate=pl.CostEstimate(
             flops=pairs * 40, bytes_accessed=pairs * 8, transcendentals=0
         ),
-    )(edge, mid, even, odd)
+    )(*edges, *mids, even, odd)
 
 
 def passed_along(value, axis, steps):
@@ -156,10 +168,11 @@
     by_row = jnp.transpose(acquired, (2, 0, 1, 3))
     edge = jnp.concatenate([by_row[:row_reach], by_row[height - row_reach :]], axis=0)
     mid = by_row[row_reach : height - row_reach]
-    edges = jnp.stack([edge] + [passed_along(edge, "date", -s) for s in range(1, SHIFTS)])
-    mids = jnp.stack([mid] + [passed_along(mid, "date", -s) for s in range(1, SHIFTS)])
+    edges = [edge] + [passed_along(edge, "date", -s) for s in range(1, SHIFTS)]
+    mids = [mid] + [passed_along(mid, "date", -s) for s in range(1, SHIFTS)]
     odd_tile = lax.rem(lax.axis_index("tile"), 2)
-    tops, bottoms = edges[:, :row_reach], edges[:, row_reach:]
+    tops = jnp.stack([e[:row_reach] for e in edges])
+    bottoms = jnp.stack([e[row_reach:] for e in edges])
     even = swapped(jnp.where(odd_tile == 0, bottoms, tops), "tile", 0)
     odd = swapped(jnp.where(odd_tile == 1, bottoms, tops), "tile", 1)
     found = coherence_of("tile", edges, mids, even, odd)

time: 32 us -> 26.7 us (0.83)
  the two profiles are of different devices: /device:TPU:17 before, /device:TPU:0 now
where the time goes in v2:
time: 26.7 us; the launch traced here: 26.5 us
  starting transfers between devices  13.2 us (49%)
  waiting for transfers between devices  8.1 us (30%)
  Pallas kernels  4.19 us (16%)
  local copies, waits for them, and re-layouts  0.98 us (4%)
    ppermute x6, starting transfers between devices, passed_along(): return lax.ppermute(value, axis, pairs)  11.5 us
    ppermute x6, waiting for transfers between devices, passed_along(): return lax.ppermute(value, axis, pairs)  8.1 us
    pallas_call x1, Pallas kernels, coherence_of(): pl.pallas_call(body, out_shape=jax.ShapeDtypeStruct(result, jnp.float32),...  4.19 us
    ppermute x2, starting transfers between devices, swapped(): return lax.ppermute(value, axis, pairs)  1.67 us
    unnamed x1, local copies, waits for them, and re-layouts  0.95 us
  transfers between devices with their start and end apart: 8, of which 6 were waited for; matrix products, arithmetic and copies ran while one was open for 0% of the time, Pallas kernels for 0%

profile of v2, /device:TPU:0, one launch (start us, length us, event | category | flops | bytes accessed | tf_op | source)
XLA Modules:
  0.0 26.5 jit_solution(17825044652048209821)
XLA Ops:
  0.0 0.9 %copy.4 = f32[2,8,16,128]{3,1,0,2:T(8,128)S(1)} copy(f32[2,8,16,128]{3,2,1,0:T(8,128)} %param.1) | data formatting | bytes 262144 | tf_op args[0]
  1.0 3.1 %collective-permute-start.2 = (f32[10,2,8,128]{3,2,1,0:T(8,128)S(1)}, f32[10,2,8,128]{3,2,1,0:T(8,128)S(1)}, u32[]{:S(2)}, u32[]{:S(2)}) collective-permute-start(f32[10,2,8,128]{3,2,1,0:T(8,128)S(1)} %pad_maximum_fusion.2.refs_0_), channel_id=1, source_target_pairs={{0,4},{4,8},{8,12},{12,0},{1,5},{5,9},{9,13},{13,1},{2,6},{6,10},{... | collective-permute-start | bytes 245768 | tf_op jit(solution)/shard_map/ppermute | solution.py:153
  4.1 2.6 %collective-permute-start.1 = (f32[10,2,8,128]{3,2,1,0:T(8,128)S(1)}, f32[10,2,8,128]{3,2,1,0:T(8,128)S(1)}, u32[]{:S(2)}, u32[]{:S(2)}) collective-permute-start(f32[10,2,8,128]{3,2,1,0:T(8,128)S(1)} %pad_maximum_fusion.2.refs_0_), channel_id=1, source_target_pairs={{0,8},{4,12},{8,0},{12,4},{1,9},{5,13},{9,1},{13,5},{2,10},{6,14},... | collective-permute-start | bytes 245768 | tf_op jit(solution)/shard_map/ppermute | solution.py:153
  6.7 1.3 %collective-permute-start = (f32[10,2,8,128]{3,2,1,0:T(8,128)S(1)}, f32[10,2,8,128]{3,2,1,0:T(8,128)S(1)}, u32[]{:S(2)}, u32[]{:S(2)}) collective-permute-start(f32[10,2,8,128]{3,2,1,0:T(8,128)S(1)} %pad_maximum_fusion.2.refs_0_), channel_id=1, source_target_pairs={{0,12},{4,0},{8,4},{12,8},{1,13},{5,1},{9,5},{13,9},{2,14},{6,2},{... | collective-permute-start | bytes 245768 | tf_op jit(solution)/shard_map/ppermute | solution.py:153
  8.0 1.0 %collective-permute-done.2.refs_3_ = f32[10,2,8,128]{3,2,1,0:T(8,128)S(1)} collective-permute-done((f32[10,2,8,128]{3,2,1,0:T(8,128)S(1)}, f32[10,2,8,128]{3,2,1,0:T(8,128)S(1)}, u32[]{:S(2)}, u32[]{:S(2)}) %collective-permute-start.2) | collective-permute-done | bytes 81952 | tf_op jit(solution)/shard_map/ppermute | solution.py:153
  9.1 3.1 %collective-permute-done.1.refs_2_ = f32[10,2,8,128]{3,2,1,0:T(8,128)S(1)} collective-permute-done((f32[10,2,8,128]{3,2,1,0:T(8,128)S(1)}, f32[10,2,8,128]{3,2,1,0:T(8,128)S(1)}, u32[]{:S(2)}, u32[]{:S(2)}) %collective-permute-start.1) | collective-permute-done | bytes 81952 | tf_op jit(solution)/shard_map/ppermute | solution.py:153
  12.2 0.2 collective-permute-done.refs_1_
  12.4 0.8 %collective-permute-start.7 = (f32[4,5,2,8,128]{4,3,2,1,0:T(8,128)S(1)}, f32[4,5,2,8,128]{4,3,2,1,0:T(8,128)S(1)}, u32[]{:S(2)}, u32[]{:S(2)}) collective-permute-start(f32[4,5,2,8,128]{4,3,2,1,0:T(8,128)S(1)} %get-tuple-element.5), channel_id=1, source_target_pairs={{1,2},{2,1},{0,3},{3,0},{5,6},{6,5},{4,7},{7,4},{9,10},{10,9},{8,1... | collective-permute-start | bytes 491528 | tf_op jit(solution)/shard_map/ppermute | solution.py:163
  13.2 0.9 %collective-permute-start.6 = (f32[4,5,2,8,128]{4,3,2,1,0:T(8,128)S(1)}, f32[4,5,2,8,128]{4,3,2,1,0:T(8,128)S(1)}, u32[]{:S(2)}, u32[]{:S(2)}) collective-permute-start(f32[4,5,2,8,128]{4,3,2,1,0:T(8,128)S(1)} %get-tuple-element.6), channel_id=1, source_target_pairs={{0,1},{1,0},{2,3},{3,2},{4,5},{5,4},{6,7},{7,6},{8,9},{9,8},{10,11... | collective-permute-start | bytes 491528 | tf_op jit(solution)/shard_map/ppermute | solution.py:163
  14.1 2.0 %collective-permute-start.5 = (f32[6,2,8,128]{3,2,1,0:T(8,128)S(1)}, f32[6,2,8,128]{3,2,1,0:T(8,128)S(1)}, u32[]{:S(2)}, u32[]{:S(2)}) collective-permute-start(f32[6,2,8,128]{3,2,1,0:T(8,128)S(1)} %slice.38.refs_4_), channel_id=1, source_target_pairs={{0,4},{4,8},{8,12},{12,0},{1,5},{5,9},{9,13},{13,1},{2,6},{6,10},{... | collective-permute-start | bytes 147464 | tf_op jit(solution)/shard_map/ppermute | solution.py:153
  16.1 1.9 %collective-permute-start.4 = (f32[6,2,8,128]{3,2,1,0:T(8,128)S(1)}, f32[6,2,8,128]{3,2,1,0:T(8,128)S(1)}, u32[]{:S(2)}, u32[]{:S(2)}) collective-permute-start(f32[6,2,8,128]{3,2,1,0:T(8,128)S(1)} %slice.38.refs_4_), channel_id=1, source_target_pairs={{0,8},{4,12},{8,0},{12,4},{1,9},{5,13},{9,1},{13,5},{2,10},{6,14},... | collective-permute-start | bytes 147464 | tf_op jit(solution)/shard_map/ppermute | solution.py:153
  18.0 0.6 %collective-permute-start.3 = (f32[6,2,8,128]{3,2,1,0:T(8,128)S(1)}, f32[6,2,8,128]{3,2,1,0:T(8,128)S(1)}, u32[]{:S(2)}, u32[]{:S(2)}) collective-permute-start(f32[6,2,8,128]{3,2,1,0:T(8,128)S(1)} %slice.38.refs_4_), channel_id=1, source_target_pairs={{0,12},{4,0},{8,4},{12,8},{1,13},{5,1},{9,5},{13,9},{2,14},{6,2},{... | collective-permute-start | bytes 147464 | tf_op jit(solution)/shard_map/ppermute | solution.py:153
  18.6 1.7 %collective-permute-done.5.refs_7_ = f32[6,2,8,128]{3,2,1,0:T(8,128)S(1)} collective-permute-done((f32[6,2,8,128]{3,2,1,0:T(8,128)S(1)}, f32[6,2,8,128]{3,2,1,0:T(8,128)S(1)}, u32[]{:S(2)}, u32[]{:S(2)}) %collective-permute-start.5) | collective-permute-done | bytes 49184 | tf_op jit(solution)/shard_map/ppermute | solution.py:153
  20.3 1.6 %collective-permute-done.4.refs_6_ = f32[6,2,8,128]{3,2,1,0:T(8,128)S(1)} collective-permute-done((f32[6,2,8,128]{3,2,1,0:T(8,128)S(1)}, f32[6,2,8,128]{3,2,1,0:T(8,128)S(1)}, u32[]{:S(2)}, u32[]{:S(2)}) %collective-permute-start.4) | collective-permute-done | bytes 49184 | tf_op jit(solution)/shard_map/ppermute | solution.py:153
  21.9 0.4 %collective-permute-done.3.refs_5_ = f32[6,2,8,128]{3,2,1,0:T(8,128)S(1)} collective-permute-done((f32[6,2,8,128]{3,2,1,0:T(8,128)S(1)}, f32[6,2,8,128]{3,2,1,0:T(8,128)S(1)}, u32[]{:S(2)}, u32[]{:S(2)}) %collective-permute-start.3) | collective-permute-done | bytes 49184 | tf_op jit(solution)/shard_map/ppermute | solution.py:153
  22.3 0.0 collective-permute-done.7.refs_9_
  22.3 0.0 collective-permute-done.6.refs_8_
  22.3 4.2 %shard_map.17 = f32[2,4,8,128,128]{4,3,2,1,0:T(8,128)} custom-call(f32[10,2,8,128]{3,2,1,0:T(8,128)S(1)} %pad_maximum_fusion.2.refs_0_, f32[10,2,8,128]{3,2,1,0:T(8,128)S(1)} %collective-permute-done.refs_1_, f32[10,2,8,128]{3,2,1,0:T(8,128)S(1)} %collective-permute-done.1.refs_2_, f32[10,2,8,128]{3,2,1,0:T(8,128)S(1)} %collective-permute-done.2.refs_3_, ...), custom_call_target="tpu_custom_call" | custom-call | flops 20971520 | bytes 4194304 | tf_op jit(solution)/shard_map/pallas_call | solution.py:132
  (7 shorter events, 0.1 us)
Async XLA Ops:
  1.0 8.1 %collective-permute-start.2 = (f32[10,2,8,128]{3,2,1,0:T(8,128)S(1)}, f32[10,2,8,128]{3,2,1,0:T(8,128)S(1)}, u32[]{:S(2)}, u32[]{:S(2)}) collective-permute-start(f32[10,2,8,128]{3,2,1,0:T(8,128)S(1)} %pad_maximum_fusion.2.refs_0_), channel_id=1, source_target_pairs={{0,4},{4,8},{8,12},{12,0},{1,5},{5,9},{9,13},{13,1},{2,6},{6,10},{... | collective-permute-start | bytes 245768 | tf_op jit(solution)/shard_map/ppermute | solution.py:153
  4.1 8.1 %collective-permute-start.1 = (f32[10,2,8,128]{3,2,1,0:T(8,128)S(1)}, f32[10,2,8,128]{3,2,1,0:T(8,128)S(1)}, u32[]{:S(2)}, u32[]{:S(2)}) collective-permute-start(f32[10,2,8,128]{3,2,1,0:T(8,128)S(1)} %pad_maximum_fusion.2.refs_0_), channel_id=1, source_target_pairs={{0,8},{4,12},{8,0},{12,4},{1,9},{5,13},{9,1},{13,5},{2,10},{6,14},... | collective-permute-start | bytes 245768 | tf_op jit(solution)/shard_map/ppermute | solution.py:153
  6.7 5.7 %collective-permute-start = (f32[10,2,8,128]{3,2,1,0:T(8,128)S(1)}, f32[10,2,8,128]{3,2,1,0:T(8,128)S(1)}, u32[]{:S(2)}, u32[]{:S(2)}) collective-permute-start(f32[10,2,8,128]{3,2,1,0:T(8,128)S(1)} %pad_maximum_fusion.2.refs_0_), channel_id=1, source_target_pairs={{0,12},{4,0},{8,4},{12,8},{1,13},{5,1},{9,5},{13,9},{2,14},{6,2},{... | collective-permute-start | bytes 245768 | tf_op jit(solution)/shard_map/ppermute | solution.py:153
  12.4 9.9 %collective-permute-start.7 = (f32[4,5,2,8,128]{4,3,2,1,0:T(8,128)S(1)}, f32[4,5,2,8,128]{4,3,2,1,0:T(8,128)S(1)}, u32[]{:S(2)}, u32[]{:S(2)}) collective-permute-start(f32[4,5,2,8,128]{4,3,2,1,0:T(8,128)S(1)} %get-tuple-element.5), channel_id=1, source_target_pairs={{1,2},{2,1},{0,3},{3,0},{5,6},{6,5},{4,7},{7,4},{9,10},{10,9},{8,1... | collective-permute-start | bytes 491528 | tf_op jit(solution)/shard_map/ppermute | solution.py:163
  13.2 9.1 %collective-permute-start.6 = (f32[4,5,2,8,128]{4,3,2,1,0:T(8,128)S(1)}, f32[4,5,2,8,128]{4,3,2,1,0:T(8,128)S(1)}, u32[]{:S(2)}, u32[]{:S(2)}) collective-permute-start(f32[4,5,2,8,128]{4,3,2,1,0:T(8,128)S(1)} %get-tuple-element.6), channel_id=1, source_target_pairs={{0,1},{1,0},{2,3},{3,2},{4,5},{5,4},{6,7},{7,6},{8,9},{9,8},{10,11... | collective-permute-start | bytes 491528 | tf_op jit(solution)/shard_map/ppermute | solution.py:163
  14.1 6.2 %collective-permute-start.5 = (f32[6,2,8,128]{3,2,1,0:T(8,128)S(1)}, f32[6,2,8,128]{3,2,1,0:T(8,128)S(1)}, u32[]{:S(2)}, u32[]{:S(2)}) collective-permute-start(f32[6,2,8,128]{3,2,1,0:T(8,128)S(1)} %slice.38.refs_4_), channel_id=1, source_target_pairs={{0,4},{4,8},{8,12},{12,0},{1,5},{5,9},{9,13},{13,1},{2,6},{6,10},{... | collective-permute-start | bytes 147464 | tf_op jit(solution)/shard_map/ppermute | solution.py:153
  16.1 5.8 %collective-permute-start.4 = (f32[6,2,8,128]{3,2,1,0:T(8,128)S(1)}, f32[6,2,8,128]{3,2,1,0:T(8,128)S(1)}, u32[]{:S(2)}, u32[]{:S(2)}) collective-permute-start(f32[6,2,8,128]{3,2,1,0:T(8,128)S(1)} %slice.38.refs_4_), channel_id=1, source_target_pairs={{0,8},{4,12},{8,0},{12,4},{1,9},{5,13},{9,1},{13,5},{2,10},{6,14},... | collective-permute-start | bytes 147464 | tf_op jit(solution)/shard_map/ppermute | solution.py:153
  18.0 4.3 %collective-permute-start.3 = (f32[6,2,8,128]{3,2,1,0:T(8,128)S(1)}, f32[6,2,8,128]{3,2,1,0:T(8,128)S(1)}, u32[]{:S(2)}, u32[]{:S(2)}) collective-permute-start(f32[6,2,8,128]{3,2,1,0:T(8,128)S(1)} %slice.38.refs_4_), channel_id=1, source_target_pairs={{0,12},{4,0},{8,4},{12,8},{1,13},{5,1},{9,5},{13,9},{2,14},{6,2},{... | collective-permute-start | bytes 147464 | tf_op jit(solution)/shard_map/ppermute | solution.py:153

commit v3 on v2

--- a/solution.py
+++ b/solution.py
@@ -5,7 +5,9 @@
 from jax.experimental.pallas import tpu as pltpu
 from jax.sharding import PartitionSpec as P
 
+
 SHIFTS = 4
+
 
 row_reach = 5
 col_reach = 2
@@ -42,11 +44,12 @@
 
 
 def kernel_body(blocks, axis, groups, unroll, *refs):
-    edge_refs, mid_refs = refs[:blocks], refs[blocks : 2 * blocks]
-    even_ref, odd_ref, out_ref, halo, inverse, found, sems = refs[2 * blocks :]
-    _, _, dates, breadth = edge_refs[0].shape
-    inner = mid_refs[0].shape[0]
-    height = inner + 2 * row_reach
+    outer_refs, rest_refs = refs[:blocks], refs[blocks : 2 * blocks]
+    even_ref, odd_ref, out_ref, field, inverse, found, sems = refs[2 * blocks :]
+    _, _, dates, breadth = outer_refs[0].shape
+    inner = rest_refs[0].shape[0]
+    height = inner + row_reach
+    extent = height + 2 * row_reach
     reach = 2 * row_reach + 1
     here = lax.axis_index(axis)
     count = lax.axis_size(axis)
@@ -58,25 +61,22 @@
 
     even_live = jnp.where(here == count - 1, odd_tile, 1) == 1
     odd_live = jnp.where(odd_tile == 0, here > 0, here < count - 1)
+    odd_at = odd_tile * (height + row_reach)
+    even_at = (1 - odd_tile) * (height + row_reach)
+    outer_at = row_reach + odd_tile * inner
+    rest_at = (2 - odd_tile) * row_reach
     for k in range(blocks):
         even = even_ref[k]
         odd = odd_ref[k]
-        halo[k, 1 - odd_tile] = jnp.where(even_live, even, jnp.zeros_like(even))
-        halo[k, odd_tile] = jnp.where(odd_live, odd, jnp.zeros_like(odd))
+        field[k, pl.ds(even_at, row_reach)] = jnp.where(even_live, even, jnp.zeros_like(even))
+        field[k, pl.ds(odd_at, row_reach)] = jnp.where(odd_live, odd, jnp.zeros_like(odd))
+        field[k, pl.ds(outer_at, row_reach)] = outer_refs[k][...]
+        field[k, pl.ds(rest_at, inner)] = rest_refs[k][...]
 
     def row(k, r, part, date=None):
         at = slice(None) if date is None else pl.ds(date, 1)
-        if r < row_reach:
-            return halo[k, 0, r, part, at, :]
-        if r < 2 * row_reach:
-            return edge_refs[k][r - row_reach, part, at, :]
-        if r < 2 * row_reach + inner:
-            return mid_refs[k][r - 2 * row_reach, part, at, :]
-        if r < 3 * row_reach + inner:
-            return edge_refs[k][r - row_reach - inner, part, at, :]
-        return halo[k, 1, r - 3 * row_reach - inner, part, at, :]
+        return field[k, r, part, at, :]
 
-    extent = height + 2 * row_reach
     for k in range(blocks):
         squares = []
         for r in range(extent):
@@ -119,10 +119,10 @@
         copy.wait()
 
 
-def coherence_of(axis, edges, mids, even, odd, groups=2, unroll=4):
-    blocks = len(edges)
-    _, _, dates, breadth = edges[0].shape
-    height = mids[0].shape[0] + 2 * row_reach
+def coherence_of(axis, outers, rests, even, odd, groups=2, unroll=4):
+    blocks = len(outers)
+    _, _, dates, breadth = outers[0].shape
+    height = rests[0].shape[0] + row_reach
 
     def body(*refs):
         kernel_body(blocks, axis, groups, unroll, *refs)
@@ -135,7 +135,7 @@
         in_specs=[pl.BlockSpec(memory_space=pltpu.VMEM)] * (2 * blocks + 2),
         out_specs=pl.BlockSpec(memory_space=pl.ANY),
         scratch_shapes=[
-            pltpu.VMEM((blocks, 2, row_reach, 2, dates, breadth), jnp.float32),
+            pltpu.VMEM((blocks, height + 2 * row_reach, 2, dates, breadth), jnp.float32),
             pltpu.VMEM((blocks, height, dates, breadth), jnp.float32),
             pltpu.VMEM(result, jnp.float32),
             pltpu.SemaphoreType.DMA((blocks, groups, 2)),
@@ -144,7 +144,7 @@
         cost_estimate=pl.CostEstimate(
             flops=pairs * 40, bytes_accessed=pairs * 8, transcendentals=0
         ),
-    )(*edges, *mids, even, odd)
+    )(*outers, *rests, even, odd)
 
 
 def passed_along(value, axis, steps):
@@ -166,16 +166,19 @@
 def on_device(acquired):
     height = acquired.shape[2]
     by_row = jnp.transpose(acquired, (2, 0, 1, 3))
-    edge = jnp.concatenate([by_row[:row_reach], by_row[height - row_reach :]], axis=0)
-    mid = by_row[row_reach : height - row_reach]
-    edges = [edge] + [passed_along(edge, "date", -s) for s in range(1, SHIFTS)]
-    mids = [mid] + [passed_along(mid, "date", -s) for s in range(1, SHIFTS)]
-    odd_tile = lax.rem(lax.axis_index("tile"), 2)
-    tops = jnp.stack([e[:row_reach] for e in edges])
-    bottoms = jnp.stack([e[row_reach:] for e in edges])
-    even = swapped(jnp.where(odd_tile == 0, bottoms, tops), "tile", 0)
-    odd = swapped(jnp.where(odd_tile == 1, bottoms, tops), "tile", 1)
-    found = coherence_of("tile", edges, mids, even, odd)
+    odd_tile = lax.rem(lax.axis_index("tile"), 2) == 1
+    head, tail = by_row[:row_reach], by_row[height - row_reach :]
+    outer = jnp.where(odd_tile, tail, head)
+    rest = jnp.where(odd_tile, by_row[: height - row_reach], by_row[row_reach:])
+    outers, rests = [outer], [rest]
+    for s in range(1, SHIFTS):
+        outers.append(passed_along(outer, "date", -s))
+        rests.append(passed_along(rest, "date", -s))
+    inner = height - 2 * row_reach
+    odd = swapped(jnp.stack(outers), "tile", 1)
+    near = [jnp.where(odd_tile, r[:row_reach], r[inner:]) for r in rests]
+    even = swapped(jnp.stack(near), "tile", 0)
+    found = coherence_of("tile", outers, rests, even, odd)
     parts, shifts, dates = found.shape[:3]
     return found.reshape(parts, shifts, dates, dates, height, found.shape[-1])
 

time: 26.7 us -> 23.2 us (0.87)
  starting transfers between devices: 13.2 us -> 11.1 us
  waiting for transfers between devices: 8.1 us -> 6.64 us
    ppermute x6, waiting for transfers between devices: 8.1 us -> 5.26 us  [passed_along(): return lax.ppermute(value, axis, pairs)]
    ppermute x2, starting transfers between devices: 1.67 us -> 0.14 us  [swapped(): return lax.ppermute(value, axis, pairs)]
    ppermute x2, waiting for transfers between devices: 0.01 us -> 1.38 us  [swapped(): return lax.ppermute(value, axis, pairs)]
    ppermute x6, starting transfers between devices: 11.5 us -> 11 us  [passed_along(): return lax.ppermute(value, axis, pairs)]
  transfers between devices with their start and end apart: 8 -> 8, of which waited for: 6 -> 4; matrix products, arithmetic and copies ran while one was open for 0% -> 0% of each run, Pallas kernels for 0% -> 0%
where the time goes in v3:
time: 23.2 us; the launch traced here: 23.1 us
  starting transfers between devices  11.1 us (48%)
  waiting for transfers between devices  6.64 us (29%)
  Pallas kernels  4.21 us (18%)
  local copies, waits for them, and re-layouts  0.95 us (4%)
    ppermute x6, starting transfers between devices, passed_along(): return lax.ppermute(value, axis, pairs)  11 us
    ppermute x6, waiting for transfers between devices, passed_along(): return lax.ppermute(value, axis, pairs)  5.26 us
    pallas_call x1, Pallas kernels, coherence_of(): pl.pallas_call(body, out_shape=jax.ShapeDtypeStruct(result, jnp.float32),...  4.21 us
    ppermute x2, waiting for transfers between devices, swapped(): return lax.ppermute(value, axis, pairs)  1.38 us
    unnamed x1, local copies, waits for them, and re-layouts  0.95 us
  transfers between devices with their start and end apart: 8, of which 4 were waited for; matrix products, arithmetic and copies ran while one was open for 0% of the time, Pallas kernels for 0%

profile of v3, /device:TPU:0, one launch (start us, length us, event | category | flops | bytes accessed | tf_op | source)
XLA Modules:
  0.0 23.1 jit_solution(11933365334194680295)
XLA Ops:
  0.0 0.9 %copy.4 = f32[2,8,16,128]{3,1,0,2:T(8,128)S(1)} copy(f32[2,8,16,128]{3,2,1,0:T(8,128)} %param.1) | data formatting | bytes 262144 | tf_op args[0]
  1.0 3.1 %collective-permute-start.2 = (f32[5,2,8,128]{3,2,1,0:T(8,128)S(1)}, f32[5,2,8,128]{3,2,1,0:T(8,128)S(1)}, u32[]{:S(2)}, u32[]{:S(2)}) collective-permute-start(f32[5,2,8,128]{3,2,1,0:T(8,128)S(1)} %slice_select_fusion.5.refs_0_), channel_id=1, source_target_pairs={{0,4},{4,8},{8,12},{12,0},{1,5},{5,9},{9,13},{13,1},{2,6},{6,10},{... | collective-permute-start | bytes 122888 | tf_op jit(solution)/shard_map/ppermute | solution.py:153
  4.1 2.6 %collective-permute-start.1 = (f32[5,2,8,128]{3,2,1,0:T(8,128)S(1)}, f32[5,2,8,128]{3,2,1,0:T(8,128)S(1)}, u32[]{:S(2)}, u32[]{:S(2)}) collective-permute-start(f32[5,2,8,128]{3,2,1,0:T(8,128)S(1)} %slice_select_fusion.5.refs_0_), channel_id=1, source_target_pairs={{0,8},{4,12},{8,0},{12,4},{1,9},{5,13},{9,1},{13,5},{2,10},{6,14},... | collective-permute-start | bytes 122888 | tf_op jit(solution)/shard_map/ppermute | solution.py:153
  6.7 1.3 %collective-permute-start = (f32[5,2,8,128]{3,2,1,0:T(8,128)S(1)}, f32[5,2,8,128]{3,2,1,0:T(8,128)S(1)}, u32[]{:S(2)}, u32[]{:S(2)}) collective-permute-start(f32[5,2,8,128]{3,2,1,0:T(8,128)S(1)} %slice_select_fusion.5.refs_0_), channel_id=1, source_target_pairs={{0,12},{4,0},{8,4},{12,8},{1,13},{5,1},{9,5},{13,9},{2,14},{6,2},{... | collective-permute-start | bytes 122888 | tf_op jit(solution)/shard_map/ppermute | solution.py:153
  8.0 0.7 %collective-permute-start.5 = (f32[11,2,8,128]{3,2,1,0:T(8,128)S(1)}, f32[11,2,8,128]{3,2,1,0:T(8,128)S(1)}, u32[]{:S(2)}, u32[]{:S(2)}) collective-permute-start(f32[11,2,8,128]{3,2,1,0:T(8,128)S(1)} %slice_select_fusion.refs_4_), channel_id=1, source_target_pairs={{0,4},{4,8},{8,12},{12,0},{1,5},{5,9},{9,13},{13,1},{2,6},{6,10},{... | collective-permute-start | bytes 270344 | tf_op jit(solution)/shard_map/ppermute | solution.py:153
  8.8 0.3 %collective-permute-start.4 = (f32[11,2,8,128]{3,2,1,0:T(8,128)S(1)}, f32[11,2,8,128]{3,2,1,0:T(8,128)S(1)}, u32[]{:S(2)}, u32[]{:S(2)}) collective-permute-start(f32[11,2,8,128]{3,2,1,0:T(8,128)S(1)} %slice_select_fusion.refs_4_), channel_id=1, source_target_pairs={{0,8},{4,12},{8,0},{12,4},{1,9},{5,13},{9,1},{13,5},{2,10},{6,14},... | collective-permute-start | bytes 270344 | tf_op jit(solution)/shard_map/ppermute | solution.py:153
  9.1 0.0 collective-permute-done.2.refs_3_
  9.1 2.9 %collective-permute-start.3 = (f32[11,2,8,128]{3,2,1,0:T(8,128)S(1)}, f32[11,2,8,128]{3,2,1,0:T(8,128)S(1)}, u32[]{:S(2)}, u32[]{:S(2)}) collective-permute-start(f32[11,2,8,128]{3,2,1,0:T(8,128)S(1)} %slice_select_fusion.refs_4_), channel_id=1, source_target_pairs={{0,12},{4,0},{8,4},{12,8},{1,13},{5,1},{9,5},{13,9},{2,14},{6,2},{... | collective-permute-start | bytes 270344 | tf_op jit(solution)/shard_map/ppermute | solution.py:153
  12.0 0.0 collective-permute-done.1.refs_2_
  12.0 0.0 collective-permute-done.refs_1_
  12.0 0.1 collective-permute-start.7
  12.1 3.3 %collective-permute-done.5.refs_7_ = f32[11,2,8,128]{3,2,1,0:T(8,128)S(1)} collective-permute-done((f32[11,2,8,128]{3,2,1,0:T(8,128)S(1)}, f32[11,2,8,128]{3,2,1,0:T(8,128)S(1)}, u32[]{:S(2)}, u32[]{:S(2)}) %collective-permute-start.5) | collective-permute-done | bytes 90144 | tf_op jit(solution)/shard_map/ppermute | solution.py:153
  15.4 2.0 %collective-permute-done.4.refs_6_ = f32[11,2,8,128]{3,2,1,0:T(8,128)S(1)} collective-permute-done((f32[11,2,8,128]{3,2,1,0:T(8,128)S(1)}, f32[11,2,8,128]{3,2,1,0:T(8,128)S(1)}, u32[]{:S(2)}, u32[]{:S(2)}) %collective-permute-start.4) | collective-permute-done | bytes 90144 | tf_op jit(solution)/shard_map/ppermute | solution.py:153
  17.4 0.0 collective-permute-done.3.refs_5_
  17.4 0.1 collective-permute-start.6
  17.5 1.0 %collective-permute-done.7.refs_9_ = f32[4,5,2,8,128]{4,3,2,1,0:T(8,128)S(1)} collective-permute-done((f32[4,5,2,8,128]{4,3,2,1,0:T(8,128)S(1)}, f32[4,5,2,8,128]{4,3,2,1,0:T(8,128)S(1)}, u32[]{:S(2)}, u32[]{:S(2)}) %collective-permute-start.7) | collective-permute-done | bytes 163872 | tf_op jit(solution)/shard_map/ppermute | solution.py:163
  18.5 0.3 %collective-permute-done.6.refs_8_ = f32[4,5,2,8,128]{4,3,2,1,0:T(8,128)S(1)} collective-permute-done((f32[4,5,2,8,128]{4,3,2,1,0:T(8,128)S(1)}, f32[4,5,2,8,128]{4,3,2,1,0:T(8,128)S(1)}, u32[]{:S(2)}, u32[]{:S(2)}) %collective-permute-start.6) | collective-permute-done | bytes 163872 | tf_op jit(solution)/shard_map/ppermute | solution.py:163
  18.9 4.2 %shard_map.17 = f32[2,4,8,128,128]{4,3,2,1,0:T(8,128)} custom-call(f32[5,2,8,128]{3,2,1,0:T(8,128)S(1)} %slice_select_fusion.5.refs_0_, f32[5,2,8,128]{3,2,1,0:T(8,128)S(1)} %collective-permute-done.refs_1_, f32[5,2,8,128]{3,2,1,0:T(8,128)S(1)} %collective-permute-done.1.refs_2_, f32[5,2,8,128]{3,2,1,0:T(8,128)S(1)} %collective-permute-done.2.refs_3_, ...), custom_call_target="tpu_custom_call" | custom-call | flops 20971520 | bytes 4194304 | tf_op jit(solution)/shard_map/pallas_call | solution.py:132
  (9 shorter events, 0.1 us)
Async XLA Ops:
  1.0 8.1 %collective-permute-start.2 = (f32[5,2,8,128]{3,2,1,0:T(8,128)S(1)}, f32[5,2,8,128]{3,2,1,0:T(8,128)S(1)}, u32[]{:S(2)}, u32[]{:S(2)}) collective-permute-start(f32[5,2,8,128]{3,2,1,0:T(8,128)S(1)} %slice_select_fusion.5.refs_0_), channel_id=1, source_target_pairs={{0,4},{4,8},{8,12},{12,0},{1,5},{5,9},{9,13},{13,1},{2,6},{6,10},{... | collective-permute-start | bytes 122888 | tf_op jit(solution)/shard_map/ppermute | solution.py:153
  4.1 7.9 %collective-permute-start.1 = (f32[5,2,8,128]{3,2,1,0:T(8,128)S(1)}, f32[5,2,8,128]{3,2,1,0:T(8,128)S(1)}, u32[]{:S(2)}, u32[]{:S(2)}) collective-permute-start(f32[5,2,8,128]{3,2,1,0:T(8,128)S(1)} %slice_select_fusion.5.refs_0_), channel_id=1, source_target_pairs={{0,8},{4,12},{8,0},{12,4},{1,9},{5,13},{9,1},{13,5},{2,10},{6,14},... | collective-permute-start | bytes 122888 | tf_op jit(solution)/shard_map/ppermute | solution.py:153
  6.7 5.3 %collective-permute-start = (f32[5,2,8,128]{3,2,1,0:T(8,128)S(1)}, f32[5,2,8,128]{3,2,1,0:T(8,128)S(1)}, u32[]{:S(2)}, u32[]{:S(2)}) collective-permute-start(f32[5,2,8,128]{3,2,1,0:T(8,128)S(1)} %slice_select_fusion.5.refs_0_), channel_id=1, source_target_pairs={{0,12},{4,0},{8,4},{12,8},{1,13},{5,1},{9,5},{13,9},{2,14},{6,2},{... | collective-permute-start | bytes 122888 | tf_op jit(solution)/shard_map/ppermute | solution.py:153
  8.0 7.4 %collective-permute-start.5 = (f32[11,2,8,128]{3,2,1,0:T(8,128)S(1)}, f32[11,2,8,128]{3,2,1,0:T(8,128)S(1)}, u32[]{:S(2)}, u32[]{:S(2)}) collective-permute-start(f32[11,2,8,128]{3,2,1,0:T(8,128)S(1)} %slice_select_fusion.refs_4_), channel_id=1, source_target_pairs={{0,4},{4,8},{8,12},{12,0},{1,5},{5,9},{9,13},{13,1},{2,6},{6,10},{... | collective-permute-start | bytes 270344 | tf_op jit(solution)/shard_map/ppermute | solution.py:153
  8.8 8.6 %collective-permute-start.4 = (f32[11,2,8,128]{3,2,1,0:T(8,128)S(1)}, f32[11,2,8,128]{3,2,1,0:T(8,128)S(1)}, u32[]{:S(2)}, u32[]{:S(2)}) collective-permute-start(f32[11,2,8,128]{3,2,1,0:T(8,128)S(1)} %slice_select_fusion.refs_4_), channel_id=1, source_target_pairs={{0,8},{4,12},{8,0},{12,4},{1,9},{5,13},{9,1},{13,5},{2,10},{6,14},... | collective-permute-start | bytes 270344 | tf_op jit(solution)/shard_map/ppermute | solution.py:153
  9.1 8.2 %collective-permute-start.3 = (f32[11,2,8,128]{3,2,1,0:T(8,128)S(1)}, f32[11,2,8,128]{3,2,1,0:T(8,128)S(1)}, u32[]{:S(2)}, u32[]{:S(2)}) collective-permute-start(f32[11,2,8,128]{3,2,1,0:T(8,128)S(1)} %slice_select_fusion.refs_4_), channel_id=1, source_target_pairs={{0,12},{4,0},{8,4},{12,8},{1,13},{5,1},{9,5},{13,9},{2,14},{6,2},{... | collective-permute-start | bytes 270344 | tf_op jit(solution)/shard_map/ppermute | solution.py:153
  12.0 6.5 %collective-permute-start.7 = (f32[4,5,2,8,128]{4,3,2,1,0:T(8,128)S(1)}, f32[4,5,2,8,128]{4,3,2,1,0:T(8,128)S(1)}, u32[]{:S(2)}, u32[]{:S(2)}) collective-permute-start(f32[4,5,2,8,128]{4,3,2,1,0:T(8,128)S(1)} %pad_maximum_fusion.1), channel_id=1, source_target_pairs={{1,2},{2,1},{0,3},{3,0},{5,6},{6,5},{4,7},{7,4},{9,10},{10,9},{8,1... | collective-permute-start | bytes 491528 | tf_op jit(solution)/shard_map/ppermute | solution.py:163
  17.4 1.5 %collective-permute-start.6 = (f32[4,5,2,8,128]{4,3,2,1,0:T(8,128)S(1)}, f32[4,5,2,8,128]{4,3,2,1,0:T(8,128)S(1)}, u32[]{:S(2)}, u32[]{:S(2)}) collective-permute-start(f32[4,5,2,8,128]{4,3,2,1,0:T(8,128)S(1)} %pad_maximum_fusion), channel_id=1, source_target_pairs={{0,1},{1,0},{2,3},{3,2},{4,5},{5,4},{6,7},{7,6},{8,9},{9,8},{10,11... | collective-permute-start | bytes 491528 | tf_op jit(solution)/shard_map/ppermute | solution.py:163
